TPU v7x, 32 devices: a whole 2x2x4 slice. The times are simulated.
32 devices in a mesh: blk: 32 (over z, y, x, core).
Axes of the slice: x: 2, y: 2, z: 4, core: 2. Of those that a mesh axis runs over, the one named last changes fastest.
Arguments:
- tensor_blocks: bfloat16 [352, 32, 32, 1024], P('blk')
- block_index: int32 [352, 4], P('blk'), may hold values from 0 to 8, as said below
- starts: float32 [256, 32], P(None, 'blk'), may hold values from -6 to 6
- shifts: float32 [32], replicated, may hold values from 0.5 to 2
Outputs:
- iterate: float32 [256, 32], P(None, 'blk')
- estimate: float32 [32], P('blk')
Inputs may be any that keep to these rules, and one draw needn't show every extreme that they name: `block_index`: every sorted quadruple i <= j <= k <= l of 0 to 7 is held by exactly one slot; every other slot holds 8 in all four entries and is not used. A live slot's block is unchanged when two of its axes with equal block indices are swapped.
All inputs are finite; a program needn't handle non-finite values.
Results may differ from a plain program's by a relative error of at most 0.009.
Values sent between devices are 32-bit elements; how exact they have to be, the bound alone decides.
No kernel may reach another device: no remote copies, remote signals or barrier semaphores. Data moves between devices by JAX's collectives and lax.ppermute only.
A program may use at most 192 MiB of HBM per device.

v0:
```python
import jax
import jax.numpy as jnp
from jax import lax
from jax.sharding import PartitionSpec as P

NSIZE = 256
ITERS = 2
letters = "abcd"


def normalize(values):
    return values * lax.rsqrt(jnp.mean(values * values, axis=0) + 1e-06)


def equal_counts(indices, position):
    earlier = jnp.float32(0.0)
    same_count = jnp.float32(0.0)
    for other in range(4):
        match_value = (indices[other] == indices[position]).astype(jnp.float32)
        same_count = same_count + match_value
        if other < position:
            earlier = earlier + match_value
    return (earlier, same_count)


def factor_product(indices):
    product = jnp.float32(1.0)
    for other in range(1, 4):
        earlier, unused = equal_counts(indices, other)
        product = product * (1.0 + earlier)
    return product


def contract_axis(tensor, pieces, position):
    others = [other for other in range(4) if other != position]
    leading = others[0]
    paired = (pieces[others[1]][:, None, :] * pieces[others[2]][None, :, :]).astype(jnp.bfloat16)
    kept = "".join(sorted(letters[position] + letters[leading]))
    pattern = "abcd," + letters[others[1]] + letters[others[2]] + "r->" + kept + "r"
    partial_sum = jnp.einsum(pattern, tensor, paired, preferred_element_type=jnp.float32)
    if position < leading:
        return jnp.sum(partial_sum * pieces[leading][None, :, :], axis=1)
    return jnp.sum(partial_sum * pieces[leading][:, None, :], axis=0)


def apply_tensor(tensor_blocks, block_index, current):
    tile_size = tensor_blocks.shape[1]
    blocks_count = NSIZE // tile_size
    total = jnp.zeros(current.shape, jnp.float32)
    for slot_id in range(tensor_blocks.shape[0]):
        tensor = tensor_blocks[slot_id].reshape(tile_size, tile_size, tile_size, tile_size)
        indices = block_index[slot_id]
        live = (indices[0] < blocks_count).astype(jnp.float32)
        safe = jnp.minimum(indices, blocks_count - 1)
        pieces = [
            lax.dynamic_slice_in_dim(current, safe[other] * tile_size, tile_size, 0)
            for other in range(4)
        ]
        weight = live * 6.0 / factor_product(indices)
        for position in range(4):
            result = weight * contract_axis(tensor, pieces, position)
            start = safe[position] * tile_size
            total = lax.dynamic_update_slice_in_dim(
                total, lax.dynamic_slice_in_dim(total, start, tile_size, 0) + result, start, 0
            )
    return total


def body(tensor_blocks, block_index, starts, shifts):
    own_count = starts.shape[1]
    offset = lax.axis_index("blk") * own_count
    own_shifts = lax.dynamic_slice_in_dim(shifts, offset, own_count, 0)
    current_own = normalize(starts)
    current = lax.all_gather(current_own, "blk", axis=1, tiled=True)
    previous_own = current_own
    image_own = current_own
    for step_id in range(ITERS):
        applied = apply_tensor(tensor_blocks, block_index, current)
        final_turn = step_id == ITERS - 1
        summed = lax.psum(applied, "blk")
        image_own = lax.dynamic_slice_in_dim(summed, offset, own_count, 1)
        previous_own = lax.dynamic_slice_in_dim(current, offset, own_count, 1)
        if final_turn:
            current_own = normalize(image_own + own_shifts[None, :] * previous_own)
        else:
            current = normalize(summed + shifts[None, :] * current)
    estimate = jnp.mean(previous_own * image_own, axis=0) * lax.rsqrt(
        jnp.mean(image_own * image_own, axis=0) + 1e-06
    )
    return (current_own, estimate)


def solution(mesh):
    placed = (P("blk", None, None, None), P("blk", None), P(None, "blk"), P())
    return jax.shard_map(
        body, mesh=mesh, in_specs=placed, out_specs=(P(None, "blk"), P("blk")), check_vma=False
    )
```

profile of v0, /device:TPU:0, one launch (start us, length us, event | category | flops | bytes accessed | tf_op | source)
XLA Modules:
  0.0 739.3 jit_solution(965814484213138154)
XLA Ops:
  5.7 43.3 %all-gather = f32[32,1,256]{2,1,0:T(1,128)S(1)} all-gather(f32[1,1,256]{2,1,0:T(1,128)S(1)} %multiply_bitcast_fusion), channel_id=1, replica_groups=mesh['blk'=32] {'blk'}, dimensions={0}, use_global_device_ids=true | all-gather | bytes 33792 | tf_op jit(solution)/shard_map/all_gather | solution.py:74
  63.7 15.7 %fusion.548 = (bf16[1,32,32,1024]{3,2,1,0:T(8,128)(2,1)S(1)}, bf16[1,32,32,1024]{3,2,1,0:T(8,128)(2,1)}, bf16[1,32,32,1024]{3,2,1,0:T(8,128)(2,1)}, bf16[1,32,32...) fusion(bf16[11,32,32,1024]{3,2,1,0:T(8,128)(2,1)} %param.4), kind=kLoop, calls=%fused_computation.877 | loop fusion | bytes 46137344 | tf_op jit(solution)/shard_map/slice | solution.py:51
  79.4 10.9 %reshape_squeeze.44 = bf16[32,32,32,32]{3,2,1,0:T(8,128)(2,1)} reshape(bf16[1,32,32,1024]{3,2,1,0:T(8,128)(2,1)} %get-tuple-element.60) | data formatting | bytes 4194304 | tf_op jit(solution)/shard_map/reshape;squeeze | solution.py:51
  95.9 6.1 multiply_reduce_fusion.42
  128.8 11.3 %reshape_squeeze.45 = bf16[32,32,32,32]{3,2,1,0:T(8,128)(2,1)} reshape(bf16[1,32,32,1024]{3,2,1,0:T(8,128)(2,1)} %get-tuple-element.59) | data formatting | bytes 4194304 | tf_op jit(solution)/shard_map/reshape;squeeze | solution.py:51
  140.2 6.1 multiply_reduce_fusion.40
  161.1 11.0 %reshape_squeeze.46 = bf16[32,32,32,32]{3,2,1,0:T(8,128)(2,1)} reshape(bf16[1,32,32,1024]{3,2,1,0:T(8,128)(2,1)} %get-tuple-element.58) | data formatting | bytes 4194304 | tf_op jit(solution)/shard_map/reshape;squeeze | solution.py:51
  172.2 6.1 multiply_reduce_fusion.38
  188.6 3.6 fusion.192
  192.3 11.1 %reshape_squeeze.47 = bf16[32,32,32,32]{3,2,1,0:T(8,128)(2,1)} reshape(bf16[1,32,32,1024]{3,2,1,0:T(8,128)(2,1)} %get-tuple-element.57) | data formatting | bytes 4194304 | tf_op jit(solution)/shard_map/reshape;squeeze | solution.py:51
  203.5 6.1 multiply_reduce_fusion.36
  220.0 3.6 fusion.190
  223.7 11.1 %reshape_squeeze.48 = bf16[32,32,32,32]{3,2,1,0:T(8,128)(2,1)} reshape(bf16[1,32,32,1024]{3,2,1,0:T(8,128)(2,1)} %get-tuple-element.56) | data formatting | bytes 4194304 | tf_op jit(solution)/shard_map/reshape;squeeze | solution.py:51
  234.9 6.1 multiply_reduce_fusion.34
  255.3 11.4 %reshape_squeeze.49 = bf16[32,32,32,32]{3,2,1,0:T(8,128)(2,1)} reshape(bf16[1,32,32,1024]{3,2,1,0:T(8,128)(2,1)} %get-tuple-element.55) | data formatting | bytes 4194304 | tf_op jit(solution)/shard_map/reshape;squeeze | solution.py:51
  266.8 6.1 multiply_reduce_fusion.32
  283.3 3.6 fusion.186
  287.1 11.0 %reshape_squeeze.50 = bf16[32,32,32,32]{3,2,1,0:T(8,128)(2,1)} reshape(bf16[1,32,32,1024]{3,2,1,0:T(8,128)(2,1)} %get-tuple-element.54) | data formatting | bytes 4194304 | tf_op jit(solution)/shard_map/reshape;squeeze | solution.py:51
  298.2 6.1 multiply_reduce_fusion.30
  319.5 11.1 %reshape_squeeze.51 = bf16[32,32,32,32]{3,2,1,0:T(8,128)(2,1)} reshape(bf16[1,32,32,1024]{3,2,1,0:T(8,128)(2,1)} %get-tuple-element.53) | data formatting | bytes 4194304 | tf_op jit(solution)/shard_map/reshape;squeeze | solution.py:51
  330.6 6.1 multiply_reduce_fusion.28
  347.2 3.6 fusion.182
  350.9 11.1 %reshape_squeeze.52 = bf16[32,32,32,32]{3,2,1,0:T(8,128)(2,1)} reshape(bf16[1,32,32,1024]{3,2,1,0:T(8,128)(2,1)} %get-tuple-element.52) | data formatting | bytes 4194304 | tf_op jit(solution)/shard_map/reshape;squeeze | solution.py:51
  362.1 6.1 multiply_reduce_fusion.26
  378.9 3.6 fusion.180
  382.7 11.3 %reshape_squeeze.53 = bf16[32,32,32,32]{3,2,1,0:T(8,128)(2,1)} reshape(bf16[1,32,32,1024]{3,2,1,0:T(8,128)(2,1)} %get-tuple-element.61) | data formatting | bytes 4194304 | tf_op jit(solution)/shard_map/reshape;squeeze | solution.py:51
  394.1 6.1 multiply_reduce_fusion.24
  414.6 8.1 %reshape_squeeze.54 = bf16[32,32,32,32]{3,2,1,0:T(8,128)(2,1)} reshape(bf16[1,32,32,1024]{3,2,1,0:T(8,128)(2,1)S(1)} %get-tuple-element.51) | data formatting | bytes 4194304 | tf_op jit(solution)/shard_map/reshape;squeeze | solution.py:51
  422.7 6.1 multiply_reduce_fusion.22
  443.2 38.1 %psum.14 = f32[256,32]{1,0:T(8,128)S(1)} all-reduce(f32[256,32]{1,0:T(8,128)S(1)} %constant_dynamic-update-slice_fusion.44), channel_id=1, replica_groups=mesh['blk'=32] {'blk'}, use_global_device_ids=true, to_apply=%region_45.0 | all-reduce | flops 8192 | bytes 65536 | tf_op jit(solution)/shard_map/psum | solution.py:80
  481.6 5.9 multiply_reduce_fusion.20
  487.6 5.8 fusion.175
  493.4 6.9 fusion.174
  500.4 5.9 multiply_reduce_fusion.18
  506.3 5.8 fusion.173
  512.2 7.3 fusion.172
  519.7 5.9 multiply_reduce_fusion.16
  525.6 5.8 fusion.171
  531.5 6.9 fusion.170
  538.5 6.1 multiply_reduce_fusion.14
  544.6 5.8 fusion.169
  550.5 6.9 fusion.168
  557.5 5.9 multiply_reduce_fusion.12
  563.4 5.8 fusion.167
  569.3 7.1 fusion.166
  576.5 5.9 multiply_reduce_fusion.10
  582.4 5.8 fusion.165
  588.3 6.9 fusion.164
  595.4 5.9 multiply_reduce_fusion.8
  601.3 6.2 fusion.163
  607.6 6.9 fusion.162
  614.6 5.9 multiply_reduce_fusion.6
  620.5 5.8 fusion.161
  626.4 6.9 fusion.160
  633.4 6.1 multiply_reduce_fusion.4
  639.5 5.8 fusion.159
  645.4 6.9 fusion.158
  652.4 5.9 multiply_reduce_fusion.2
  658.3 5.8 fusion.157
  664.2 7.1 fusion.156
  671.4 5.9 multiply_reduce_fusion
  677.3 5.8 fusion.155
  683.1 6.9 fusion.154
  690.1 42.2 %psum.15 = f32[256,32]{1,0:T(8,128)S(1)} all-reduce(f32[256,32]{1,0:T(8,128)S(1)} %constant_dynamic-update-slice_fusion), channel_id=1, replica_groups=mesh['blk'=32] {'blk'}, use_global_device_ids=true, to_apply=%region_91.0 | all-reduce | flops 8192 | bytes 65536 | tf_op jit(solution)/shard_map/psum | solution.py:80
  (214 shorter events, 67.3 us)
Async XLA Ops:
  90.3 11.7 %copy-start.11 = (s32[11,4]{0,1:T(4,128)S(1)}, s32[11,4]{0,1:T(4,128)}, u32[]{:S(2)}) copy-start(s32[11,4]{0,1:T(4,128)} %param.5) | copy-start | bytes 532
  95.9 14.8 %copy-start = (bf16[32,32,32,32]{3,2,1,0:T(8,128)(2,1)S(1)}, bf16[32,32,32,32]{3,2,1,0:T(8,128)(2,1)}, u32[]{:S(2)}) copy-start(bf16[32,32,32,32]{3,2,1,0:T(8,128)(2,1)} %reshape_squeeze.44) | copy-start | bytes 6291460
  140.2 14.7 %copy-start.1 = (bf16[32,32,32,32]{3,2,1,0:T(8,128)(2,1)S(1)}, bf16[32,32,32,32]{3,2,1,0:T(8,128)(2,1)}, u32[]{:S(2)}) copy-start(bf16[32,32,32,32]{3,2,1,0:T(8,128)(2,1)} %reshape_squeeze.45) | copy-start | bytes 6291460
  172.2 14.0 %copy-start.2 = (bf16[32,32,32,32]{3,2,1,0:T(8,128)(2,1)S(1)}, bf16[32,32,32,32]{3,2,1,0:T(8,128)(2,1)}, u32[]{:S(2)}) copy-start(bf16[32,32,32,32]{3,2,1,0:T(8,128)(2,1)} %reshape_squeeze.46) | copy-start | bytes 6291460
  203.5 14.1 %copy-start.3 = (bf16[32,32,32,32]{3,2,1,0:T(8,128)(2,1)S(1)}, bf16[32,32,32,32]{3,2,1,0:T(8,128)(2,1)}, u32[]{:S(2)}) copy-start(bf16[32,32,32,32]{3,2,1,0:T(8,128)(2,1)} %reshape_squeeze.47) | copy-start | bytes 6291460
  234.9 14.3 %copy-start.4 = (bf16[32,32,32,32]{3,2,1,0:T(8,128)(2,1)S(1)}, bf16[32,32,32,32]{3,2,1,0:T(8,128)(2,1)}, u32[]{:S(2)}) copy-start(bf16[32,32,32,32]{3,2,1,0:T(8,128)(2,1)} %reshape_squeeze.48) | copy-start | bytes 6291460
  266.8 14.2 %copy-start.5 = (bf16[32,32,32,32]{3,2,1,0:T(8,128)(2,1)S(1)}, bf16[32,32,32,32]{3,2,1,0:T(8,128)(2,1)}, u32[]{:S(2)}) copy-start(bf16[32,32,32,32]{3,2,1,0:T(8,128)(2,1)} %reshape_squeeze.49) | copy-start | bytes 6291460
  298.2 15.1 %copy-start.6 = (bf16[32,32,32,32]{3,2,1,0:T(8,128)(2,1)S(1)}, bf16[32,32,32,32]{3,2,1,0:T(8,128)(2,1)}, u32[]{:S(2)}) copy-start(bf16[32,32,32,32]{3,2,1,0:T(8,128)(2,1)} %reshape_squeeze.50) | copy-start | bytes 6291460
  330.6 14.1 %copy-start.7 = (bf16[32,32,32,32]{3,2,1,0:T(8,128)(2,1)S(1)}, bf16[32,32,32,32]{3,2,1,0:T(8,128)(2,1)}, u32[]{:S(2)}) copy-start(bf16[32,32,32,32]{3,2,1,0:T(8,128)(2,1)} %reshape_squeeze.51) | copy-start | bytes 6291460
  362.1 14.4 %copy-start.8 = (bf16[32,32,32,32]{3,2,1,0:T(8,128)(2,1)S(1)}, bf16[32,32,32,32]{3,2,1,0:T(8,128)(2,1)}, u32[]{:S(2)}) copy-start(bf16[32,32,32,32]{3,2,1,0:T(8,128)(2,1)} %reshape_squeeze.52) | copy-start | bytes 6291460
  394.1 14.4 %copy-start.9 = (bf16[32,32,32,32]{3,2,1,0:T(8,128)(2,1)S(1)}, bf16[32,32,32,32]{3,2,1,0:T(8,128)(2,1)}, u32[]{:S(2)}) copy-start(bf16[32,32,32,32]{3,2,1,0:T(8,128)(2,1)} %reshape_squeeze.53) | copy-start | bytes 6291460
  422.7 14.4 %copy-start.10 = (bf16[32,32,32,32]{3,2,1,0:T(8,128)(2,1)S(1)}, bf16[32,32,32,32]{3,2,1,0:T(8,128)(2,1)}, u32[]{:S(2)}) copy-start(bf16[32,32,32,32]{3,2,1,0:T(8,128)(2,1)} %reshape_squeeze.54) | copy-start | bytes 6291460
  437.2 44.2 %copy-start.12 = (f32[32]{0:T(128)S(1)}, f32[32]{0:T(128)}, u32[]{:S(2)}) copy-start(f32[32]{0:T(128)} %param.7) | copy-start | bytes 388
where the time goes:
time: 754 us; the launch traced here: 739 us
  matrix products  338 us (45%)
  local copies, waits for them, and re-layouts  148 us (20%)
  blocking collectives  124 us (16%)
  between operations  122 us (16%)
    dot_general x66, matrix products, contract_axis(): jnp.einsum(pattern, tensor, paired, preferred_element_type=jnp.float32)  338 us
    another operation x11, local copies, waits for them, and re-layouts, apply_tensor(): tensor_blocks[slot_id].reshape(tile_size, tile_size, tile_size, tile_size)  119 us
    psum x2, blocking collectives, body(): summed = lax.psum(applied, 'blk')  80.3 us
    all_gather x1, blocking collectives, body(): current = lax.all_gather(current_own, 'blk', axis=1, tiled=True)  43.3 us
    slice x1, local copies, waits for them, and re-layouts, apply_tensor(): tensor_blocks[slot_id].reshape(tile_size, tile_size, tile_size, tile_size)  15.7 us

commit v1 on v0

--- a/solution.py
+++ b/solution.py
@@ -77,7 +77,7 @@
     for step_id in range(ITERS):
         applied = apply_tensor(tensor_blocks, block_index, current)
         final_turn = step_id == ITERS - 1
-        summed = lax.psum(applied, "blk")
+        summed = jnp.sum(lax.all_gather(applied, "blk"), axis=0)
         image_own = lax.dynamic_slice_in_dim(summed, offset, own_count, 1)
         previous_own = lax.dynamic_slice_in_dim(current, offset, own_count, 1)
         if final_turn:

time: 754 us -> 757 us (level)
  waiting for transfers between devices: 0 us -> 102 us
  blocking collectives: 124 us -> 43.3 us
  matrix products: 338 us -> 304 us
  between operations: 122 us -> 137 us
    all_gather x0 -> x2, waiting for transfers between devices: none -> 102 us  [body(): summed = jnp.sum(lax.all_gather(applied, 'blk'), axis=0)]
    psum x2 -> x0, blocking collectives: 80.3 us -> none  [body(): summed = lax.psum(applied, 'blk')]
    dot_general x66, matrix products: 338 us -> 304 us  [contract_axis(): jnp.einsum(pattern, tensor, paired, preferred_element_type=jnp.float32)]
  transfers between devices with their start and end apart: 0 -> 2, of which waited for: 0 -> 2; matrix products, arithmetic and copies ran while one was open for 0% -> 0% of each run, Pallas kernels for 0% -> 0%
where the time goes in v1:
time: 757 us; the launch traced here: 749 us
  matrix products  304 us (40%)
  local copies, waits for them, and re-layouts  154 us (20%)
  between operations  137 us (18%)
  waiting for transfers between devices  102 us (13%)
  blocking collectives  43.3 us (6%)
  other arithmetic  8.96 us (1%)
    dot_general x66, matrix products, contract_axis(): jnp.einsum(pattern, tensor, paired, preferred_element_type=jnp.float32)  304 us
    another operation x11, local copies, waits for them, and re-layouts, apply_tensor(): tensor_blocks[slot_id].reshape(tile_size, tile_size, tile_size, tile_size)  120 us
    all_gather x2, waiting for transfers between devices, body(): summed = jnp.sum(lax.all_gather(applied, 'blk'), axis=0)  102 us
    all_gather x1, blocking collectives, body(): current = lax.all_gather(current_own, 'blk', axis=1, tiled=True)  43.3 us
    slice x1, local copies, waits for them, and re-layouts, apply_tensor(): tensor_blocks[slot_id].reshape(tile_size, tile_size, tile_size, tile_size)  16.1 us
  transfers between devices with their start and end apart: 2, of which 2 were waited for; matrix products, arithmetic and copies ran while one was open for 0% of the time, Pallas kernels for 0%

profile of v1, /device:TPU:0, one launch (start us, length us, event | category | flops | bytes accessed | tf_op | source)
XLA Modules:
  0.0 749.5 jit_solution(15829074523614100602)
XLA Ops:
  136.9 43.3 %all-gather = f32[32,1,256]{2,1,0:T(1,128)S(1)} all-gather(f32[1,1,256]{2,1,0:T(1,128)S(1)} %multiply_bitcast_fusion), channel_id=1, replica_groups=mesh['blk'=32] {'blk'}, dimensions={0}, use_global_device_ids=true | all-gather | bytes 33792 | tf_op jit(solution)/shard_map/all_gather | solution.py:74
  182.3 16.1 %fusion.552 = (bf16[1,32,32,1024]{3,2,1,0:T(8,128)(2,1)S(1)}, bf16[1,32,32,1024]{3,2,1,0:T(8,128)(2,1)}, bf16[1,32,32,1024]{3,2,1,0:T(8,128)(2,1)}, bf16[1,32,32...) fusion(bf16[11,32,32,1024]{3,2,1,0:T(8,128)(2,1)} %param.4), kind=kLoop, calls=%fused_computation.882 | loop fusion | bytes 46137344 | tf_op jit(solution)/shard_map/slice | solution.py:51
  198.4 10.9 %reshape_squeeze.45 = bf16[32,32,32,32]{3,2,1,0:T(8,128)(2,1)} reshape(bf16[1,32,32,1024]{3,2,1,0:T(8,128)(2,1)} %get-tuple-element.58) | data formatting | bytes 4194304 | tf_op jit(solution)/shard_map/reshape;squeeze | solution.py:51
  209.3 7.1 fusion.194
  218.7 2.5 multiply_reduce_fusion.40
  221.4 11.4 %reshape_squeeze.44 = bf16[32,32,32,32]{3,2,1,0:T(8,128)(2,1)} reshape(bf16[1,32,32,1024]{3,2,1,0:T(8,128)(2,1)} %get-tuple-element.59) | data formatting | bytes 4194304 | tf_op jit(solution)/shard_map/reshape;squeeze | solution.py:51
  232.9 7.1 fusion.196
  242.3 2.5 multiply_reduce_fusion.42
  245.1 11.0 %reshape_squeeze.46 = bf16[32,32,32,32]{3,2,1,0:T(8,128)(2,1)} reshape(bf16[1,32,32,1024]{3,2,1,0:T(8,128)(2,1)} %get-tuple-element.57) | data formatting | bytes 4194304 | tf_op jit(solution)/shard_map/reshape;squeeze | solution.py:51
  256.2 7.1 fusion.192
  268.4 11.1 %reshape_squeeze.47 = bf16[32,32,32,32]{3,2,1,0:T(8,128)(2,1)} reshape(bf16[1,32,32,1024]{3,2,1,0:T(8,128)(2,1)} %get-tuple-element.56) | data formatting | bytes 4194304 | tf_op jit(solution)/shard_map/reshape;squeeze | solution.py:51
  279.5 7.1 fusion.190
  289.0 2.5 multiply_reduce_fusion.36
  291.8 11.1 %reshape_squeeze.48 = bf16[32,32,32,32]{3,2,1,0:T(8,128)(2,1)} reshape(bf16[1,32,32,1024]{3,2,1,0:T(8,128)(2,1)} %get-tuple-element.55) | data formatting | bytes 4194304 | tf_op jit(solution)/shard_map/reshape;squeeze | solution.py:51
  302.9 7.1 fusion.188
  312.4 2.5 multiply_reduce_fusion.34
  315.1 11.4 %reshape_squeeze.49 = bf16[32,32,32,32]{3,2,1,0:T(8,128)(2,1)} reshape(bf16[1,32,32,1024]{3,2,1,0:T(8,128)(2,1)} %get-tuple-element.54) | data formatting | bytes 4194304 | tf_op jit(solution)/shard_map/reshape;squeeze | solution.py:51
  326.5 7.1 fusion.186
  336.0 2.5 multiply_reduce_fusion.32
  338.7 11.0 %reshape_squeeze.50 = bf16[32,32,32,32]{3,2,1,0:T(8,128)(2,1)} reshape(bf16[1,32,32,1024]{3,2,1,0:T(8,128)(2,1)} %get-tuple-element.53) | data formatting | bytes 4194304 | tf_op jit(solution)/shard_map/reshape;squeeze | solution.py:51
  349.8 7.1 fusion.184
  359.2 2.5 multiply_reduce_fusion.30
  362.0 11.1 %reshape_squeeze.51 = bf16[32,32,32,32]{3,2,1,0:T(8,128)(2,1)} reshape(bf16[1,32,32,1024]{3,2,1,0:T(8,128)(2,1)} %get-tuple-element.52) | data formatting | bytes 4194304 | tf_op jit(solution)/shard_map/reshape;squeeze | solution.py:51
  373.1 7.1 fusion.182
  382.6 2.5 multiply_reduce_fusion.28
  385.4 11.1 %reshape_squeeze.52 = bf16[32,32,32,32]{3,2,1,0:T(8,128)(2,1)} reshape(bf16[1,32,32,1024]{3,2,1,0:T(8,128)(2,1)} %get-tuple-element.51) | data formatting | bytes 4194304 | tf_op jit(solution)/shard_map/reshape;squeeze | solution.py:51
  396.5 7.1 fusion.180
  406.0 2.5 multiply_reduce_fusion.26
  408.7 11.3 %reshape_squeeze.53 = bf16[32,32,32,32]{3,2,1,0:T(8,128)(2,1)} reshape(bf16[1,32,32,1024]{3,2,1,0:T(8,128)(2,1)} %get-tuple-element.60) | data formatting | bytes 4194304 | tf_op jit(solution)/shard_map/reshape;squeeze | solution.py:51
  420.1 7.1 fusion.178
  429.6 2.5 multiply_reduce_fusion.24
  432.3 8.1 %reshape_squeeze.54 = bf16[32,32,32,32]{3,2,1,0:T(8,128)(2,1)} reshape(bf16[1,32,32,1024]{3,2,1,0:T(8,128)(2,1)S(1)} %get-tuple-element.50) | data formatting | bytes 4194304 | tf_op jit(solution)/shard_map/reshape;squeeze | solution.py:51
  440.4 7.1 fusion.176
  449.9 2.5 multiply_reduce_fusion.22
  454.9 49.6 %all-gather.4.cloned.1.call-done = f32[32,256,32]{1,2,0:T(8,128)} async-done(((f32[1,256,32]{1,2,0:T(8,128)}), f32[32,256,32]{1,2,0:T(8,128)}) %all-gather.4.cloned.1.call-update) | async-done | bytes 1048592 | tf_op jit(solution)/shard_map/all_gather | solution.py:80
  506.8 7.1 fusion.154
  513.9 5.9 fusion.155
  519.9 2.5 multiply_reduce_fusion
  522.6 7.1 fusion.156
  529.7 6.3 fusion.157
  536.1 2.5 multiply_reduce_fusion.2
  538.8 7.1 fusion.158
  545.9 5.9 fusion.159
  554.6 7.2 fusion.160
  561.8 5.9 fusion.161
  567.8 2.5 multiply_reduce_fusion.6
  570.5 7.1 fusion.162
  577.6 5.9 fusion.163
  583.6 2.7 multiply_reduce_fusion.8
  586.5 7.1 fusion.164
  593.6 5.9 fusion.165
  599.6 2.5 multiply_reduce_fusion.10
  602.3 7.5 fusion.166
  609.8 5.9 fusion.167
  615.7 2.5 multiply_reduce_fusion.12
  618.5 7.1 fusion.168
  625.6 5.9 fusion.169
  634.2 7.2 fusion.170
  641.5 5.9 fusion.171
  650.1 7.1 fusion.172
  657.2 6.2 fusion.173
  666.2 7.1 fusion.174
  673.3 5.9 fusion.175
  683.9 52.2 %all-gather.6.cloned.1.call-done = f32[32,256,32]{1,2,0:T(8,128)} async-done(((f32[1,256,32]{1,2,0:T(8,128)}), f32[32,256,32]{1,2,0:T(8,128)}) %all-gather.6.cloned.1.call-update) | async-done | bytes 1048592 | tf_op jit(solution)/shard_map/all_gather | solution.py:80
  (290 shorter events, 69.1 us)
Async XLA Ops:
  7.2 497.3 %all-gather.4.cloned.1.call-start = ((), (), s32[]{:S(2)}) async-start(), calls=%async_computation | async-start | bytes 1081344 | tf_op jit(solution)/shard_map/all_gather | solution.py:80
  180.2 18.2 %copy-start.11 = (f32[32,1,256]{2,1,0:T(1,128)}, f32[32,1,256]{2,1,0:T(1,128)S(1)}, u32[]{:S(2)}) copy-start(f32[32,1,256]{2,1,0:T(1,128)S(1)} %all-gather) | copy-start | bytes 98308
  209.3 7.1 copy-start.1
  232.9 7.1 copy-start
  256.2 7.1 copy-start.2
  279.5 7.1 copy-start.3
  302.9 7.1 copy-start.4
  326.5 7.1 copy-start.5
  349.8 7.1 copy-start.6
  373.1 7.1 copy-start.7
  396.5 7.1 copy-start.8
  420.1 7.1 copy-start.9
  440.4 7.1 copy-start.10
  449.9 55.9 %copy-start.12 = (f32[32,1,256]{2,1,0:T(1,128)S(1)}, f32[32,1,256]{2,1,0:T(1,128)}, u32[]{:S(2)}) copy-start(f32[32,1,256]{2,1,0:T(1,128)} %copy-done.11) | copy-start | bytes 98308
  449.9 55.9 %copy-start.13 = (f32[32]{0:T(128)S(1)}, f32[32]{0:T(128)}, u32[]{:S(2)}) copy-start(f32[32]{0:T(128)} %param.7) | copy-start | bytes 388
  454.6 281.4 %all-gather.6.cloned.1.call-start = ((), (), s32[]{:S(2)}) async-start(), calls=%async_computation.1 | async-start | bytes 1081344 | tf_op jit(solution)/shard_map/all_gather | solution.py:80
  506.8 13.0 %slice-start.20 = ((s8[8388608]{0:T(1024)(128)(4,1)}), s8[4194304]{0:T(1024)(128)(4,1)S(1)}, s32[]{:S(2)}) async-start(s8[8388608]{0:T(1024)(128)(4,1)} %bitcast.1075), calls=%async_computation.22 | async-start | bytes 8388608
  513.9 5.9 slice-start.21
  522.6 13.4 %slice-start.18 = ((s8[8388608]{0:T(1024)(128)(4,1)}), s8[4194304]{0:T(1024)(128)(4,1)S(1)}, s32[]{:S(2)}) async-start(s8[8388608]{0:T(1024)(128)(4,1)} %bitcast.1073), calls=%async_computation.20 | async-start | bytes 8388608
  529.7 6.4 slice-start.19
  538.8 13.0 %slice-start.16 = ((s8[8388608]{0:T(1024)(128)(4,1)}), s8[4194304]{0:T(1024)(128)(4,1)S(1)}, s32[]{:S(2)}) async-start(s8[8388608]{0:T(1024)(128)(4,1)} %bitcast.1071), calls=%async_computation.18 | async-start | bytes 8388608
  545.9 5.9 slice-start.17
  554.6 13.2 %slice-start.14 = ((s8[8388608]{0:T(1024)(128)(4,1)}), s8[4194304]{0:T(1024)(128)(4,1)S(1)}, s32[]{:S(2)}) async-start(s8[8388608]{0:T(1024)(128)(4,1)} %bitcast.1069), calls=%async_computation.16 | async-start | bytes 8388608
  561.8 5.9 slice-start.15
  570.5 13.0 %slice-start.12 = ((s8[8388608]{0:T(1024)(128)(4,1)}), s8[4194304]{0:T(1024)(128)(4,1)S(1)}, s32[]{:S(2)}) async-start(s8[8388608]{0:T(1024)(128)(4,1)} %bitcast.1067), calls=%async_computation.14 | async-start | bytes 8388608
  577.6 5.9 slice-start.13
  586.5 13.0 %slice-start.10 = ((s8[8388608]{0:T(1024)(128)(4,1)}), s8[4194304]{0:T(1024)(128)(4,1)S(1)}, s32[]{:S(2)}) async-start(s8[8388608]{0:T(1024)(128)(4,1)} %bitcast.1065), calls=%async_computation.12 | async-start | bytes 8388608
  593.6 5.9 slice-start.11
  602.3 13.4 %slice-start.8 = ((s8[8388608]{0:T(1024)(128)(4,1)}), s8[4194304]{0:T(1024)(128)(4,1)S(1)}, s32[]{:S(2)}) async-start(s8[8388608]{0:T(1024)(128)(4,1)} %bitcast.1063), calls=%async_computation.10 | async-start | bytes 8388608
  609.8 5.9 slice-start.9
  618.5 13.0 %slice-start.6 = ((s8[8388608]{0:T(1024)(128)(4,1)}), s8[4194304]{0:T(1024)(128)(4,1)S(1)}, s32[]{:S(2)}) async-start(s8[8388608]{0:T(1024)(128)(4,1)} %bitcast.1061), calls=%async_computation.8 | async-start | bytes 8388608
  625.5 5.9 slice-start.7
  634.2 13.2 %slice-start.4 = ((s8[8388608]{0:T(1024)(128)(4,1)}), s8[4194304]{0:T(1024)(128)(4,1)S(1)}, s32[]{:S(2)}) async-start(s8[8388608]{0:T(1024)(128)(4,1)} %bitcast.1059), calls=%async_computation.6 | async-start | bytes 8388608
  641.5 5.9 slice-start.5
  650.1 13.3 %slice-start.2 = ((s8[8388608]{0:T(1024)(128)(4,1)}), s8[4194304]{0:T(1024)(128)(4,1)S(1)}, s32[]{:S(2)}) async-start(s8[8388608]{0:T(1024)(128)(4,1)} %bitcast.1057), calls=%async_computation.4 | async-start | bytes 8388608
  657.2 6.2 slice-start.3
  666.2 13.0 %slice-start = ((s8[8388608]{0:T(1024)(128)(4,1)}), s8[4194304]{0:T(1024)(128)(4,1)S(1)}, s32[]{:S(2)}) async-start(s8[8388608]{0:T(1024)(128)(4,1)} %bitcast.1055), calls=%async_computation.2 | async-start | bytes 8388608
  673.2 5.9 slice-start.1
Sparse Core Ops, SparseCore 0:
  454.8 49.6 all-gather.3
  683.5 52.5 all-gather.5
